TPU v7x, 32 devices: a whole 2x2x4 slice. The times are simulated.
32 devices in a mesh: ops: 8 (over z, y), site: 4 (over x, core).
Axes of the slice: x: 2, y: 2, z: 4, core: 2. Of those that a mesh axis runs over, the one named last changes fastest.
Arguments:
- wavefunction: bfloat16 [2048, 2048], replicated, may hold values from -6 to 6
- left_blocks: bfloat16 [64, 16, 192, 192], P('ops', 'site'), may hold values from -0.4375 to 0.4375
- right_blocks: bfloat16 [64, 16, 192, 192], P('ops', 'site'), may hold values from -0.15625 to 0.15625
- left_sector: int32 [2048], replicated, may hold values from 0 to 15, as said below
- right_sector: int32 [2048], replicated, may hold values from 0 to 15, as said below
- term_count: int32 [8], P('ops'), may hold values from 1 to 8, as said below
- left_energy: float32 [2048], replicated, may hold values from -1 to 1
- right_energy: float32 [2048], replicated, may hold values from -1 to 1
- subspace: bfloat16 [2, 16, 192, 2048], P(None, 'site'), may hold values from -0.0078125 to 0.0078125
Outputs:
- sigma: bfloat16 [16, 192, 2048], P('site')
- projections: float32 [2], replicated
Inputs may be any that keep to these rules, and one draw needn't show every extreme that they name: `left_sector`: sector ids never fall along the bond; each of the 16 sectors has 1 to 192 states and one has exactly 192. `right_sector`: sector ids never fall along the bond; each of the 16 sectors has 1 to 192 states and one has exactly 192. `term_count`: some group has all 8 slots live.
All inputs are finite; a program needn't handle non-finite values.
Results may differ from a plain program's by a relative error of at most 0.0045.
Values may be sent and summed in bfloat16 or wider, within the bound.
A program may use at most 192 MiB of HBM per device.

v0:
```python
import functools

import jax
import jax.numpy as jnp
from jax import lax
from jax.experimental import pallas as pl
from jax.experimental.pallas import tpu as pltpu
from jax.sharding import PartitionSpec as P

LANE = 128
MESH = pl.DeviceIdType.MESH


def sector_tables(sector_ids, sectors):
    labels = jnp.arange(sectors, dtype=jnp.int32)
    sector_starts = jnp.sum((sector_ids[None, :] < labels[:, None]).astype(jnp.int32), axis=1)
    sector_sizes = jnp.sum((sector_ids[None, :] == labels[:, None]).astype(jnp.int32), axis=1)
    return (sector_starts, sector_sizes)


def round_up(value, step):
    return (value + step - 1) // step * step


def apply_kernel(
    slots, sec_dev, widest, wide,
    left_ref, spread_ref, right_ref,
    out_ref,
    psi_pad, images, right_pad, arrived, added,
    pair_s, pair_r, outer_s, outer_r, fwd_s, fwd_r, out_s,
):
    me = lax.axis_index("site")
    row = me // 2
    side = me % 2
    peer = row * 2 + 1 - side
    across = (1 - row) * 2 + side
    far = (1 - row) * 2 + 1 - side
    pairs = slots // 2
    shift = wide - widest

    barrier = pltpu.get_barrier_semaphore()
    for other in (peer, across):
        pl.semaphore_signal(barrier, inc=1, device_id={"site": other}, device_id_type=MESH)
    pl.semaphore_wait(barrier, 2)

    def to_pair(w):
        return pltpu.make_async_remote_copy(
            src_ref=right_ref.at[w], dst_ref=arrived.at[0, w], send_sem=pair_s.at[w],
            recv_sem=pair_r.at[w], device_id={"site": peer}, device_id_type=MESH,
        )

    def to_across(w):
        return pltpu.make_async_remote_copy(
            src_ref=right_ref.at[w], dst_ref=arrived.at[1, w], send_sem=outer_s.at[w],
            recv_sem=outer_r.at[w], device_id={"site": across}, device_id_type=MESH,
        )

    def forward(w):
        return pltpu.make_async_remote_copy(
            src_ref=arrived.at[1, w], dst_ref=arrived.at[2, w], send_sem=fwd_s.at[w],
            recv_sem=fwd_r.at[w], device_id={"site": peer}, device_id_type=MESH,
        )

    for w in range(sec_dev):
        to_across(w).start()
    for w in range(sec_dev):
        to_pair(w).start()
    right_pad[...] = jnp.zeros_like(right_pad)
    lane_in = lax.broadcasted_iota(jnp.int32, (wide, wide), 0)
    lane_out = lax.broadcasted_iota(jnp.int32, (wide, wide), 1)
    moved = (lane_in + shift == lane_out).astype(jnp.bfloat16)

    def keep(slot, sector):
        return pltpu.make_async_copy(added.at[slot], out_ref.at[sector], out_s.at[slot])

    def one_sector(i, carry):
        @pl.when((i % 3 == 0) & (i > 0) & (i <= 3 * sec_dev))
        def _():
            w = i // 3 - 1
            to_across(w).wait_recv()
            forward(w).start()

        @pl.when(i < sec_dev)
        def _():
            right_pad[0:widest, :] = right_ref[jnp.minimum(i, sec_dev - 1)]

        @pl.when((i >= sec_dev) & (i < 2 * sec_dev))
        def _():
            w = jnp.clip(i - sec_dev, 0, sec_dev - 1)
            to_pair(w).wait_recv()
            right_pad[0:widest, :] = arrived[0, w]

        later = jnp.maximum(i - 2 * sec_dev, 0)
        late_w = later // 2

        @pl.when((i >= 2 * sec_dev) & (i % 2 == 0))
        def _():
            right_pad[0:widest, :] = arrived[1, late_w]

        @pl.when((i >= 2 * sec_dev) & (i % 2 == 1))
        def _():
            forward(late_w).wait_recv()
            right_pad[0:widest, :] = arrived[2, late_w]

        early = i < 2 * sec_dev
        owner = jnp.where(
            early,
            jnp.where(i < sec_dev, me, peer),
            jnp.where(i % 2 == 0, across, far),
        )
        sector = owner * sec_dev + jnp.where(early, i % sec_dev, late_w)
        psi_pad[0] = spread_ref[sector]
        psi_pad[1] = jnp.dot(
            spread_ref[sector], moved, preferred_element_type=jnp.float32
        ).astype(jnp.bfloat16)
        for within in range(sec_dev):
            at = within * widest
            even, odd = (
                jnp.dot(
                    left_ref[within, parity],
                    psi_pad[parity, at : at + widest, :],
                    preferred_element_type=jnp.float32,
                ).astype(jnp.bfloat16)
                for parity in range(2)
            )
            for p in range(pairs):
                rows = slice(p * widest, (p + 1) * widest)
                base = 2 * p * widest
                images[at : at + widest, base : base + LANE] = even[rows, :LANE]
                images[at : at + widest, base + LANE : base + 2 * LANE] = (
                    even[rows, LANE:] + odd[rows, :LANE]
                )
                images[at : at + widest, base + 2 * LANE : base + 3 * LANE] = odd[rows, LANE:]
        slot = i % 2

        @pl.when(i >= 2)
        def _():
            keep(slot, sector).wait()

        added[slot] = lax.dot_general(
            images[...], right_pad[...], (((1,), (1,)), ((), ())), preferred_element_type=jnp.float32
        )
        keep(slot, sector).start()
        return carry

    lax.fori_loop(0, 4 * sec_dev, one_sector, 0)
    for slot in range(2):
        keep(slot, 0).wait()
    for w in range(sec_dev):
        to_pair(w).wait_send()
        to_across(w).wait_send()
        forward(w).wait_send()


def spread_kernel(wide, window, starts, sizes, slab_ref, spread_ref):
    step = pl.program_id(0)
    start = starts[step]
    size_now = sizes[step]
    first = pl.multiple_of(start // LANE * LANE, LANE)
    offset = start - first
    place = lax.broadcasted_iota(jnp.int32, (window, wide), 0)
    column = lax.broadcasted_iota(jnp.int32, (window, wide), 1)
    pick = ((place == column + offset) & (column < size_now)).astype(jnp.bfloat16)
    spread_ref[0] = jnp.dot(
        slab_ref[:, pl.ds(first, window)], pick, preferred_element_type=jnp.float32
    ).astype(jnp.bfloat16)


def place_kernel(
    widest, wide, window, starts, sizes, added_ref, vectors_ref, part_ref, corr_ref, summed
):
    step = pl.program_id(0)
    rows, bond_dim = part_ref.shape

    @pl.when(step == 0)
    def _():
        summed[...] = jnp.zeros_like(summed)

    start = starts[step]
    size_now = sizes[step]
    first = pl.multiple_of(start // LANE * LANE, LANE)
    offset = start - first
    place = lax.broadcasted_iota(jnp.int32, (window, wide), 0)
    column = lax.broadcasted_iota(jnp.int32, (window, wide), 1)
    pick = ((place == column + offset) & (column < size_now)).astype(jnp.bfloat16)
    added = added_ref[0]
    high = added.astype(jnp.bfloat16)
    low = (added - high.astype(jnp.float32)).astype(jnp.bfloat16)
    back = (((1,), (1,)), ((), ()))
    summed[:, pl.ds(first, window)] += lax.dot_general(
        high, pick, back, preferred_element_type=jnp.float32
    ) + lax.dot_general(low, pick, back, preferred_element_type=jnp.float32)

    @pl.when(step == pl.num_programs(0) - 1)
    def _():
        chunk = 16
        vectors = vectors_ref.shape[0]

        def fold(idx, totals):
            at = pl.multiple_of(idx * chunk, chunk)
            values = summed[pl.ds(at, chunk), 0:bond_dim]
            part_ref[pl.ds(at, chunk), :] = values.astype(jnp.bfloat16)
            new = []
            for k in range(vectors):
                product = vectors_ref[k, pl.ds(at, chunk), :].astype(jnp.float32) * values
                folded = product[0:8] + product[8:16]
                pieces = [folded[:, c : c + LANE] for c in range(0, bond_dim, LANE)]
                while len(pieces) > 1:
                    pieces = [a + b for a, b in zip(pieces[0::2], pieces[1::2])]
                new.append(totals[k] + pieces[0])
            return tuple(new)

        totals = lax.fori_loop(
            0, rows // chunk, fold, tuple(jnp.zeros((8, LANE), jnp.float32) for _ in range(vectors))
        )
        for k in range(vectors):
            corr_ref[k] = totals[k]


def exchange_kernel(
    groups, sites,
    part_ref, psi_ref, left_e_ref, right_e_ref, corr_ref,
    out_ref, corr_out,
    pair_in, sending, outer_in, corr_ops, corr_sites,
    pair_s, pair_r, outer_s, outer_r, gath_s, gath_r, fwd_s, fwd_r, ops_s, ops_r, site_s, site_r,
):
    outer = groups // 2
    me = lax.axis_index("ops")
    here = lax.axis_index("site")
    row = me // 2
    side = me % 2
    peer = row * 2 + 1 - side
    rows, bond_dim = part_ref.shape[1], part_ref.shape[2]
    step = 256

    barrier = pltpu.get_barrier_semaphore()
    for k in range(1, groups):
        pl.semaphore_signal(
            barrier, inc=1, device_id={"ops": lax.rem(me + k, groups)}, device_id_type=MESH
        )
    for k in range(1, sites):
        pl.semaphore_signal(
            barrier, inc=1, device_id={"site": lax.rem(here + k, sites)}, device_id_type=MESH
        )
    pl.semaphore_wait(barrier, groups - 1 + sites - 1)

    def remote(src, dst, send_sem, recv_sem, target):
        return pltpu.make_async_remote_copy(
            src_ref=src, dst_ref=dst, send_sem=send_sem, recv_sem=recv_sem,
            device_id=target, device_id_type=MESH,
        )

    halves = 2
    width = bond_dim // halves
    parts = [pl.ds(h * width, width) for h in range(halves)]

    pair = []
    for h in range(halves):
        for k in range(outer):
            dest = lax.rem(row + k + 1, outer)
            copy = remote(
                part_ref.at[dest * 2 + 1 - side, :, parts[h]], pair_in.at[k, :, parts[h]],
                pair_s.at[h, k], pair_r.at[h, k], {"ops": peer},
            )
            copy.start()
            pair.append(copy)

    corr_copies = []
    for k in range(1, groups):
        copy = remote(
            corr_ref, corr_ops.at[k], ops_s.at[k], ops_r.at[k], {"ops": lax.rem(me + k, groups)}
        )
        copy.start()
        corr_copies.append(copy)
    corr_ops[0] = corr_ref[...]

    sends = []
    for h in range(halves):
        for k in range(outer - 1):
            dest = lax.rem(row + k + 1, outer)
            mine = dest * 2 + side
            pair[h * outer + k].wait_recv()

            def add(c, carry, k=k, mine=mine, h=h):
                cols = pl.ds(pl.multiple_of(h * width + c * step, step), step)
                sending[k, :, cols] = (
                    part_ref[mine, :, cols].astype(jnp.float32)
                    + pair_in[k, :, cols].astype(jnp.float32)
                ).astype(jnp.bfloat16)
                return carry

            lax.fori_loop(0, width // step, add, 0)
            copy = remote(
                sending.at[k, :, parts[h]], outer_in.at[k, :, parts[h]],
                outer_s.at[h, k], outer_r.at[h, k], {"ops": mine},
            )
            copy.start()
            sends.append(copy)

    gathers = []
    forwards = []
    for h in range(halves):
        pair[h * outer + outer - 1].wait_recv()
        for copy in sends[h * (outer - 1) : (h + 1) * (outer - 1)]:
            copy.wait_recv()

        def finish(c, carry, h=h):
            cols = pl.ds(pl.multiple_of(h * width + c * step, step), step)
            total = part_ref[me, :, cols].astype(jnp.float32) + pair_in[
                outer - 1, :, cols
            ].astype(jnp.float32)
            for k in range(outer - 1):
                total = total + outer_in[k, :, cols].astype(jnp.float32)
            total = total + (left_e_ref[...] + right_e_ref[:, cols]) * psi_ref[:, cols].astype(
                jnp.float32
            )
            out_ref[me, :, cols] = total.astype(jnp.bfloat16)
            return carry

        lax.fori_loop(0, width // step, finish, 0)
        block = out_ref.at[me, :, parts[h]]
        for k in range(outer - 1):
            dest = lax.rem(row + k + 1, outer)
            copy = remote(
                block, block, gath_s.at[h, k], gath_r.at[h, k], {"ops": dest * 2 + side}
            )
            copy.start()
            gathers.append(copy)
        copy = remote(
            block, block, fwd_s.at[h, outer - 1], fwd_r.at[h, outer - 1], {"ops": peer}
        )
        copy.start()
        forwards.append(copy)

    for copy in corr_copies:
        copy.wait_recv()

    def corr_add(g, total):
        return total + corr_ops[lax.rem(me - g + groups, groups)]

    corr_sites[0] = lax.fori_loop(0, groups, corr_add, jnp.zeros(corr_ref.shape, jnp.float32))
    site_copies = []
    for k in range(1, sites):
        copy = remote(
            corr_sites.at[0], corr_sites.at[k], site_s.at[k], site_r.at[k],
            {"site": lax.rem(here + k, sites)},
        )
        copy.start()
        site_copies.append(copy)

    for h in range(halves):
        for k in range(outer - 1):
            source = lax.rem(row - k - 1 + outer, outer)
            block = out_ref.at[source * 2 + side, :, parts[h]]
            remote(block, block, gath_s.at[h, k], gath_r.at[h, k], {"ops": peer}).wait_recv()
            copy = remote(block, block, fwd_s.at[h, k], fwd_r.at[h, k], {"ops": peer})
            copy.start()
            forwards.append(copy)

    for copy in site_copies:
        copy.wait_recv()

    def site_add(g, total):
        return total + corr_sites[lax.rem(here - g + sites, sites)]

    corr_out[...] = lax.fori_loop(0, sites, site_add, jnp.zeros(corr_ref.shape, jnp.float32))

    for h in range(halves):
        block = out_ref.at[peer, :, parts[h]]
        remote(
            block, block, fwd_s.at[h, outer - 1], fwd_r.at[h, outer - 1], {"ops": peer}
        ).wait_recv()
        for k in range(outer - 1):
            source = lax.rem(row - k - 1 + outer, outer)
            block = out_ref.at[source * 2 + 1 - side, :, parts[h]]
            remote(block, block, fwd_s.at[h, k], fwd_r.at[h, k], {"ops": peer}).wait_recv()
    for copy in pair + corr_copies + sends + gathers + forwards + site_copies:
        copy.wait_send()


def local(
    wavefunction,
    left_blocks,
    right_blocks,
    left_sector,
    right_sector,
    term_count,
    left_energy,
    right_energy,
    subspace,
):
    slots, sec_dev, widest = left_blocks.shape[0], left_blocks.shape[1], left_blocks.shape[2]
    bond_dim = wavefunction.shape[0]
    vectors = subspace.shape[0]
    rows = sec_dev * widest
    sites = lax.axis_size("site")
    groups = lax.axis_size("ops")
    sectors = sec_dev * sites
    wide = round_up(widest, 256)
    window = round_up(widest + LANE - 1, LANE)
    padded_cols = round_up(bond_dim, LANE) - LANE + window

    assert sites == 4 and slots % 2 == 0 and 2 * (wide - widest) == LANE and wide == 2 * LANE
    right = right_blocks.transpose(1, 2, 0, 3).reshape(sec_dev, widest, slots * widest)

    left_start, left_size = sector_tables(left_sector, sectors)
    right_start, right_size = sector_tables(right_sector, sectors)
    first_sector = lax.axis_index("site") * sec_dev
    psi_padded = jnp.pad(wavefunction, ((0, widest), (0, padded_cols - bond_dim)))
    energy_padded = jnp.pad(left_energy, (0, widest))
    slabs = []
    energies = []
    insides = []
    for within in range(sec_dev):
        row_start = left_start[first_sector + within]
        inside = jnp.arange(widest, dtype=jnp.int32) < left_size[first_sector + within]
        slab = lax.dynamic_slice_in_dim(psi_padded, row_start, widest, 0)
        slabs.append(jnp.where(inside[:, None], slab, jnp.zeros((), slab.dtype)))
        energies.append(lax.dynamic_slice_in_dim(energy_padded, row_start, widest, 0))
        insides.append(inside)
    slab = jnp.concatenate(slabs, axis=0)
    energy = jnp.concatenate(energies)
    inside = jnp.stack(insides)
    live = jnp.arange(slots, dtype=jnp.int32) < term_count[0]
    keep = live[:, None, None, None] & inside[None, :, :, None] & inside[None, :, None, :]
    left = jnp.where(keep, left_blocks, jnp.zeros((), left_blocks.dtype))
    left = left.reshape(slots // 2, 2, sec_dev, widest, widest).transpose(2, 1, 0, 3, 4)
    left = left.reshape(sec_dev, 2, slots // 2 * widest, widest)
    vectors_flat = subspace.reshape(vectors, rows, bond_dim)

    own = lax.axis_index("ops")
    psi_mine = slab[:, :bond_dim]
    diagonal = (energy[:, None] + right_energy[None, :]) * psi_mine.astype(jnp.float32)
    first_group = jnp.where(own == 0, jnp.float32(1.0), jnp.float32(0.0))
    corr_diag = first_group * jnp.sum(
        vectors_flat.astype(jnp.float32) * diagonal[None], axis=(1, 2)
    )

    vmem = pl.BlockSpec(memory_space=pltpu.VMEM)
    smem = pl.BlockSpec(memory_space=pltpu.SMEM)
    dma = pltpu.SemaphoreType.DMA
    spread = pl.pallas_call(
        functools.partial(spread_kernel, wide, window),
        grid=(sectors,),
        out_shape=jax.ShapeDtypeStruct((sectors, rows, wide), jnp.bfloat16),
        in_specs=[smem, smem, vmem],
        out_specs=pl.BlockSpec((1, rows, wide), lambda step: (step, 0, 0)),
        compiler_params=pltpu.CompilerParams(
            dimension_semantics=("arbitrary",), vmem_limit_bytes=40 * 1024 * 1024
        ),
        name="spread_columns",
    )(right_start, right_size, slab)
    added = pl.pallas_call(
        functools.partial(apply_kernel, slots, sec_dev, widest, wide),
        out_shape=jax.ShapeDtypeStruct((sectors, rows, wide), jnp.float32),
        in_specs=[vmem, vmem, vmem],
        out_specs=pl.BlockSpec(memory_space=pl.ANY),
        scratch_shapes=[
            pltpu.VMEM((2, rows, wide), jnp.bfloat16),
            pltpu.VMEM((rows, slots * widest), jnp.bfloat16),
            pltpu.VMEM((wide, slots * widest), jnp.bfloat16),
            pltpu.VMEM((3, sec_dev, widest, slots * widest), jnp.bfloat16),
            pltpu.VMEM((2, rows, wide), jnp.float32),
            dma((sec_dev,)), dma((sec_dev,)),
            dma((sec_dev,)), dma((sec_dev,)),
            dma((sec_dev,)), dma((sec_dev,)),
            dma((2,)),
        ],
        compiler_params=pltpu.CompilerParams(
            collective_id=1, has_side_effects=True, vmem_limit_bytes=60 * 1024 * 1024
        ),
        name="apply_terms",
    )(left, spread, right)
    part, corr = pl.pallas_call(
        functools.partial(place_kernel, widest, wide, window),
        grid=(sectors,),
        out_shape=(
            jax.ShapeDtypeStruct((rows, bond_dim), jnp.bfloat16),
            jax.ShapeDtypeStruct((vectors, 8, LANE), jnp.float32),
        ),
        in_specs=[smem, smem, pl.BlockSpec((1, rows, wide), lambda step: (step, 0, 0)), vmem],
        out_specs=(vmem, vmem),
        scratch_shapes=[pltpu.VMEM((rows, padded_cols), jnp.float32)],
        compiler_params=pltpu.CompilerParams(
            dimension_semantics=("arbitrary",), vmem_limit_bytes=60 * 1024 * 1024
        ),
        name="place_columns",
    )(right_start, right_size, added, vectors_flat)

    share = rows // groups
    corr_mine = jnp.sum(corr, axis=(1, 2)) + corr_diag
    corr_tile = jnp.broadcast_to(corr_mine[:, None, None], (vectors, 8, LANE))
    psi_share = lax.dynamic_slice_in_dim(psi_mine, own * share, share, 0)
    energy_share = lax.dynamic_slice_in_dim(energy, own * share, share, 0)[:, None]
    outer = groups // 2
    sigma, corr_all = pl.pallas_call(
        functools.partial(exchange_kernel, groups, sites),
        out_shape=(
            jax.ShapeDtypeStruct((groups, share, bond_dim), jnp.bfloat16),
            jax.ShapeDtypeStruct((vectors, 8, LANE), jnp.float32),
        ),
        in_specs=[vmem] * 5,
        out_specs=(vmem, vmem),
        scratch_shapes=[
            pltpu.VMEM((outer, share, bond_dim), jnp.bfloat16),
            pltpu.VMEM((max(outer - 1, 1), share, bond_dim), jnp.bfloat16),
            pltpu.VMEM((max(outer - 1, 1), share, bond_dim), jnp.bfloat16),
            pltpu.VMEM((groups, vectors, 8, LANE), jnp.float32),
            pltpu.VMEM((sites, vectors, 8, LANE), jnp.float32),
            dma((2, outer)), dma((2, outer)),
            dma((2, outer)), dma((2, outer)),
            dma((2, outer)), dma((2, outer)),
            dma((2, outer)), dma((2, outer)),
            dma((groups,)), dma((groups,)),
            dma((sites,)), dma((sites,)),
        ],
        compiler_params=pltpu.CompilerParams(
            collective_id=0, has_side_effects=True, vmem_limit_bytes=60 * 1024 * 1024
        ),
        name="exchange_rows",
    )(
        part.reshape(groups, share, bond_dim),
        psi_share,
        energy_share,
        right_energy[None, :],
        corr_tile,
    )
    return (sigma.reshape(sec_dev, widest, bond_dim), corr_all[:, 0, 0])


def solution(mesh):
    in_specs = (
        P(),
        P("ops", "site", None, None),
        P("ops", "site", None, None),
        P(),
        P(),
        P("ops"),
        P(),
        P(),
        P(None, "site", None, None),
    )
    out_specs = (P("site", None, None), P())
    return jax.shard_map(local, mesh=mesh, in_specs=in_specs, out_specs=out_specs, check_vma=False)
```

profile of v0, /device:TPU:0, one launch (start us, length us, event | category | flops | bytes accessed | tf_op | source)
XLA Modules:
  0.0 248.4 jit_solution(990889842234190729)
XLA Ops:
  1.3 0.8 convert_reduce_fusion
  2.1 0.7 fusion.4
  10.5 0.6 iota_compare_fusion.6
  11.1 0.6 iota_compare_fusion.10
  11.8 0.6 iota_compare_fusion.5
  12.4 0.6 iota_compare_fusion.9
  13.0 0.6 iota_compare_fusion.4
  13.7 0.6 iota_compare_fusion.8
  14.3 0.6 iota_compare_fusion.7
  14.9 0.6 iota_compare_fusion.11
  15.6 0.8 convert_reduce_fusion.2
  16.4 0.9 pad_dynamic-slice_fusion.7
  17.6 0.7 copy.19.left_e_ref
  18.3 3.5 %and_select_fusion = bf16[8,4,192,192]{3,2,1,0:T(8,128)(2,1)S(1)} fusion(bf16[8,4,192,192]{3,2,1,0:T(8,128)(2,1)} %param.10, pred[4,192]{1,0:T(4,128)(4,1)S(1)} %pad_add_fusion, pred[8,4,192]{2,1,0:T(4,128)(4,1)S(1)} %broadcast_and_fusion), kind=kLoop, calls=%fused_computation.6 | loop fusion | flops 2359296 | bytes 4725504 | tf_op jit(solution)/shard_map/jit(_where)/select_n | solution.py:426
  21.9 2.0 copy.17
  23.8 1.8 copy.18
  25.6 3.8 %reshape.93.right_ref = bf16[4,192,1536]{2,1,0:T(8,128)(2,1)} reshape(bf16[4,192,8,192]{3,2,1,0:T(8,128)(2,1)S(1)} %copy.18) | data formatting | bytes 4718592 | tf_op jit(solution)/shard_map/reshape | solution.py:404
  29.4 3.1 %fusion = (bf16[192,2304]{1,0:T(8,128)(2,1)S(1)}, bf16[192,2304]{1,0:T(8,128)(2,1)S(1)}, bf16[192,2304]{1,0:T(8,128)(2,1)S(1)}, bf16[192,2304]{1,0:T(8,128)(2,1)S(1)}) fusion(s32[]{:T(128)S(6)} %select_n.62, bf16[2048,2048]{1,0:T(8,128)(2,1)} %param.9, pred[192]{0:T(512)(128)(4,1)S(1)} %iota_compare_fusion.7, s32[]{:T(128)S(6)} %select_n.64, ...), kind=kLoop, calls=%fused_computation.8 | loop fusion | flops 1769472 | bytes 11928336 | tf_op jit(solution)/shard_map/jit(_where)/select_n | solution.py:418
  32.6 0.3 pad_maximum_fusion.slab_ref
  32.9 0.4 slice.8
  33.3 0.8 constant_dynamic-slice_fusion.psi_ref
  34.1 3.3 %convert_multiply_fusion = f32[768,2048]{1,0:T(8,128)} fusion(f32[2048]{0:T(1024)S(1)} %copy-done.4, f32[768]{0:T(1024)S(1)} %pad_maximum_fusion.1, bf16[768,2304]{1,0:T(8,128)(2,1)S(1)} %pad_maximum_fusion.slab_ref), kind=kLoop, calls=%fused_computation.5 | loop fusion | flops 4718592 | bytes 9448448 | tf_op jit(solution)/shard_map/mul | solution.py:433
  37.4 6.4 %multiply_reduce_fusion = f32[2]{0:T(128)S(1)} fusion(bf16[2,4,192,2048]{3,2,1,0:T(8,128)(2,1)} %param.17, f32[4,192,2048]{2,1,0:T(8,128)} %bitcast.24), kind=kLoop, calls=%fused_computation | loop fusion | flops 9437182 | bytes 12582920 | tf_op jit(solution)/shard_map/reduce_sum | solution.py:435
  43.9 6.7 %spread_columns.1.spread_ref = bf16[16,768,256]{2,1,0:T(8,128)(2,1)S(1)} custom-call(s32[16]{0:T(128)S(1)} %get-tuple-element.13.starts, s32[16]{0:T(128)S(1)} %get-tuple-element.12.sizes, bf16[768,2304]{1,0:T(8,128)(2,1)S(1)} %pad_maximum_fusion.slab_ref), custom_call_target="tpu_custom_call" | custom-call | tf_op jit(solution)/shard_map/spread_columns/pallas_call | solution.py:442
  50.6 2.6 %copy-done = bf16[16,768,256]{2,1,0:T(8,128)(2,1)} copy-done((bf16[16,768,256]{2,1,0:T(8,128)(2,1)}, bf16[16,768,256]{2,1,0:T(8,128)(2,1)S(1)}, u32[]{:S(2)}) %copy-start) | copy-done | bytes 6291480
  53.2 73.0 %apply_terms.1.added_ref = f32[16,768,256]{2,1,0:T(8,128)} custom-call(bf16[4,2,768,192]{3,2,1,0:T(8,128)(2,1)} %bitcast.26, bf16[16,768,256]{2,1,0:T(8,128)(2,1)} %copy-done, bf16[4,192,1536]{2,1,0:T(8,128)(2,1)} %reshape.93.right_ref), custom_call_target="tpu_custom_call" | custom-call | tf_op jit(solution)/shard_map/apply_terms/pallas_call | solution.py:453
  126.2 21.1 %place_columns.1 = (bf16[768,2048]{1,0:T(8,128)(2,1)}, f32[2,8,128]{2,1,0:T(8,128)}) custom-call(s32[16]{0:T(128)} %copy-done.2, s32[16]{0:T(128)} %copy-done.1, f32[16,768,256]{2,1,0:T(8,128)} %apply_terms.1.added_ref, bf16[2,768,2048]{2,1,0:T(8,128)(2,1)} %bitcast.25), custom_call_target="tpu_custom_call" | custom-call | tf_op jit(solution)/shard_map/place_columns/pallas_call | solution.py:474
  147.3 0.8 reduce_sum.58
  148.1 0.7 broadcast_in_dim.72.corr_ref
  148.8 94.3 %exchange_rows.1 = (bf16[8,96,2048]{2,1,0:T(8,128)(2,1)}, f32[2,8,128]{2,1,0:T(8,128)}) custom-call(bf16[8,96,2048]{2,1,0:T(8,128)(2,1)} %bitcast.29, bf16[96,2048]{1,0:T(8,128)(2,1)} %constant_dynamic-slice_fusion.psi_ref, f32[96,1]{1,0:T(8,128)} %copy.19.left_e_ref, f32[1,2048]{1,0:T(1,128)} %bitcast.31, f32[2,8,128]{2,1,0:T(8,128)} %broadcast_in_dim.72.corr_ref), custom_call_target="tpu_custom_call" | custom-call | tf_op jit(solution)/shard_map/exchange_rows/pallas_call | solution.py:496
  243.1 1.3 slice_reduce_fusion
  244.4 4.0 %copy.22 = bf16[4,192,2048]{2,1,0:T(8,128)(2,1)} copy(bf16[4,192,2048]{2,1,0:T(8,128)(2,1)} %bitcast.30) | data formatting | bytes 6291456
  (15 shorter events, 0.3 us)
Async XLA Ops:
  16.4 27.5 %copy-start.1 = (s32[16]{0:T(128)}, s32[16]{0:T(128)S(1)}, u32[]{:S(2)}) copy-start(s32[16]{0:T(128)S(1)} %get-tuple-element.12.sizes) | copy-start | bytes 196
  16.4 27.5 %copy-start.2 = (s32[16]{0:T(128)}, s32[16]{0:T(128)S(1)}, u32[]{:S(2)}) copy-start(s32[16]{0:T(128)S(1)} %get-tuple-element.13.starts) | copy-start | bytes 196
  18.3 5.5 %copy-start.3 = (bf16[8,4,192,192]{3,2,1,0:T(8,128)(2,1)S(1)}, bf16[8,4,192,192]{3,2,1,0:T(8,128)(2,1)}, u32[]{:S(2)}) copy-start(bf16[8,4,192,192]{3,2,1,0:T(8,128)(2,1)} %param.11) | copy-start | bytes 7077892
  32.5 1.6 copy-start.4
  50.6 2.6 %copy-start = (bf16[16,768,256]{2,1,0:T(8,128)(2,1)}, bf16[16,768,256]{2,1,0:T(8,128)(2,1)S(1)}, u32[]{:S(2)}) copy-start(bf16[16,768,256]{2,1,0:T(8,128)(2,1)S(1)} %spread_columns.1.spread_ref) | copy-start | bytes 18874372
where the time goes:
time: 249 us; the launch traced here: 248 us
  Pallas kernels  195 us (78%)
  other arithmetic  24.4 us (10%)
  local copies, waits for them, and re-layouts  19.8 us (8%)
  between operations  9.08 us (4%)
    pallas_call x1, Pallas kernels, local(): pl.pallas_call(functools.partial(exchange_kernel, groups, sites), out_sha...  94.3 us
    pallas_call x1, Pallas kernels, local(): pl.pallas_call(functools.partial(apply_kernel, slots, sec_dev, widest, wi...  73 us
    pallas_call x1, Pallas kernels, local(): pl.pallas_call(functools.partial(place_kernel, widest, wide, window), gri...  21.1 us
    pallas_call x1, Pallas kernels, local(): pl.pallas_call(functools.partial(spread_kernel, wide, window), grid=(sect...  6.75 us
    unnamed x11, local copies, waits for them, and re-layouts  6.59 us
    reduce_sum x1, other arithmetic, local(): jnp.sum(vectors_flat.astype(jnp.float32) * diagonal[None], axis=(1, 2))  6.42 us
    lt x8, other arithmetic, local(): jnp.arange(widest, dtype=jnp.int32) < left_size[first_sector + within]  5.02 us

commit v1 on v0

v1 whole, which is shorter than its diff:
```python
import functools

import jax
import jax.numpy as jnp
from jax import lax
from jax.experimental import pallas as pl
from jax.experimental.pallas import tpu as pltpu
from jax.sharding import PartitionSpec as P

LANE = 128
MESH = pl.DeviceIdType.MESH
CHUNK = 256


def round_up(value, step):
    return (value + step - 1) // step * step


def step_kernel(
    groups, sites,
    tables, count, left_hbm, right_hbm, psi_hbm, vec_hbm, share_hbm, left_e_ref, right_e_ref,
    out_ref, corr_out,
    left, right, psi, vec, vec_share, slab, psi_share, e_share,
    rbuf, right_pad, psi_pad, images, terms, spread, placed, pick,
    part, pair_in, sending, outer_in, acc, corr_mine, corr_ops, corr_sites,
    load_s, pair_s, pair_r, x_s, x_r, xf_s, xf_r,
    y_s, y_r, outer_s, outer_r, gath_s, gath_r, fwd_s, fwd_r, ops_s, ops_r, site_s, site_r,
):
    half_slots, _, sec_dev, widest, _ = left.shape
    slots = 2 * half_slots
    rows = slab.shape[1]
    bond_dim = psi.shape[2]
    vectors = vec.shape[0]
    sectors = sec_dev * sites
    wide = psi_pad.shape[2]
    shift = wide - widest
    window = round_up(widest + LANE - 1, LANE)
    outer = groups // 2
    share = rows // groups
    chunks = bond_dim // CHUNK
    tiles = bond_dim // LANE
    half_sectors = sectors // 2
    half_cols = slots * widest // 2
    outside = -(-(bond_dim - CHUNK - 2 * (widest - 1)) // widest)
    overlap = min(sectors, sectors - outside)

    here = lax.axis_index("site")
    me = lax.axis_index("ops")
    xs = here // 2
    core = here % 2
    peer_site = xs * 2 + 1 - core
    across = (1 - xs) * 2 + core
    row = me // 2
    side = me % 2
    peer = row * 2 + 1 - side

    def sector_of(n):
        return jnp.where(xs == 0, n, sectors - 1 - n)

    def base_of(c):
        return pl.multiple_of(jnp.where(xs == 0, c * CHUNK, bond_dim - (c + 1) * CHUNK), CHUNK)

    def order_of(w):
        return jnp.where(xs == 0, here * sec_dev + w, sectors - 1 - here * sec_dev - w)

    def remote(src, dst, send_sem, recv_sem, target):
        return pltpu.make_async_remote_copy(
            src_ref=src, dst_ref=dst, send_sem=send_sem, recv_sem=recv_sem,
            device_id=target, device_id_type=MESH,
        )

    loads = [
        pltpu.make_async_copy(right_hbm, right, load_s.at[0]),
        pltpu.make_async_copy(left_hbm, left, load_s.at[1]),
        pltpu.make_async_copy(psi_hbm, psi, load_s.at[2]),
        pltpu.make_async_copy(share_hbm.at[:, me], vec_share, load_s.at[3]),
    ]
    for k in range(vectors):
        for t in range(tiles):
            loads.append(
                pltpu.make_async_copy(
                    vec_hbm.at[k, :, t * LANE : (t + 1) * LANE], vec.at[k, t],
                    load_s.at[4 + k * tiles + t],
                )
            )
    for load in loads:
        load.start()

    barrier = pltpu.get_barrier_semaphore()
    for k in range(1, groups):
        pl.semaphore_signal(
            barrier, inc=1, device_id={"ops": lax.rem(me + k, groups)}, device_id_type=MESH
        )
    for k in range(1, sites):
        pl.semaphore_signal(
            barrier, inc=1, device_id={"site": lax.rem(here + k, sites)}, device_id_type=MESH
        )

    lane_in = lax.broadcasted_iota(jnp.int32, (widest, wide), 0)
    lane_out = lax.broadcasted_iota(jnp.int32, (widest, wide), 1)
    lower = (lane_in == lane_out).astype(jnp.bfloat16)
    upper = (lane_in + shift == lane_out).astype(jnp.bfloat16)

    loads[0].wait()

    def pack(w, carry):
        n = order_of(w)
        for p in range(half_slots):
            even = jnp.dot(
                right[2 * p, w], lower, preferred_element_type=jnp.float32
            ).astype(jnp.bfloat16)
            odd = jnp.dot(
                right[2 * p + 1, w], upper, preferred_element_type=jnp.float32
            ).astype(jnp.bfloat16)
            at = 2 * p * widest
            rbuf[n, :, at : at + LANE] = even[:, :LANE]
            rbuf[n, :, at + LANE : at + 2 * LANE] = even[:, LANE:] + odd[:, :LANE]
            rbuf[n, :, at + 2 * LANE : at + 3 * LANE] = odd[:, LANE:]
        return carry

    lax.fori_loop(0, sec_dev, pack, 0)
    pl.semaphore_wait(barrier, groups - 1 + sites - 1)

    def to_pair(n):
        return remote(
            rbuf.at[n], rbuf.at[n], pair_s.at[n], pair_r.at[n], {"site": peer_site}
        )

    my_half = pl.ds(pl.multiple_of(core * half_cols, half_cols), half_cols)
    peer_half = pl.ds(pl.multiple_of((1 - core) * half_cols, half_cols), half_cols)

    def to_across(n):
        far_n = sectors - 1 - n
        return remote(
            rbuf.at[n, :, my_half], rbuf.at[far_n, :, my_half],
            x_s.at[n], x_r.at[far_n - half_sectors], {"site": across},
        )

    def forward(n, columns):
        return remote(
            rbuf.at[n, :, columns], rbuf.at[n, :, columns],
            xf_s.at[n - half_sectors], xf_r.at[n - half_sectors], {"site": peer_site},
        )

    def start_pair(w, carry):
        to_pair(order_of(w)).start()
        return carry

    lax.fori_loop(0, sec_dev, start_pair, 0)

    def start_across(idx, carry):
        n = half_sectors - 1 - idx
        owner = sector_of(n) // sec_dev

        @pl.when(owner != here)
        def _():
            to_pair(n).wait_recv()

        to_across(n).start()
        return carry

    lax.fori_loop(0, half_sectors, start_across, 0)

    first_sector = here * sec_dev

    span = window // LANE

    def window_of(start):
        first = jnp.minimum(start // LANE, tiles - span)
        return first, start - first * LANE

    right_pad[...] = jnp.zeros_like(right_pad)
    placed[...] = jnp.zeros_like(placed)
    acc[...] = jnp.zeros_like(acc)

    loads[1].wait()
    live_count = count[0]
    row_at = lax.broadcasted_iota(jnp.int32, (widest, widest), 0)
    for q in range(sec_dev):
        size_now = tables[1, first_sector + q]
        inside = row_at < size_now

        def mask(p, carry, q=q, inside=inside):
            for parity in range(2):
                keep = inside & (row_at * 0 + (2 * p + parity) < live_count)
                left[p, parity, q] = jnp.where(
                    keep, left[p, parity, q].astype(jnp.float32), 0.0
                ).astype(jnp.bfloat16)
            return carry

        lax.fori_loop(0, half_slots, mask, 0)

    loads[2].wait()
    for q in range(sec_dev):
        first, offset = window_of(tables[0, first_sector + q])
        out_row = lax.broadcasted_iota(jnp.int32, (widest, window), 0)
        in_row = lax.broadcasted_iota(jnp.int32, (widest, window), 1)
        size_now = tables[1, first_sector + q]
        choose = ((in_row == out_row + offset) & (out_row < size_now)).astype(jnp.bfloat16)
        found = jnp.dot(
            choose, jnp.concatenate([psi[first + t] for t in range(span)], axis=0),
            preferred_element_type=jnp.float32,
        ).astype(jnp.bfloat16)
        for t in range(tiles):
            slab[t, q * widest : (q + 1) * widest, :] = found[:, t * LANE : (t + 1) * LANE]

    share_at = me * share
    share_q = first_sector + share_at // widest
    share_off = share_at % widest
    first, offset = window_of(tables[0, share_q])
    out_row = lax.broadcasted_iota(jnp.int32, (share, window), 0) + share_off
    in_row = lax.broadcasted_iota(jnp.int32, (share, window), 1)
    share_mask = (in_row == out_row + offset) & (out_row < tables[1, share_q])
    choose = share_mask.astype(jnp.bfloat16)
    psi_share[...] = jnp.dot(
        choose, jnp.concatenate([psi[first + t] for t in range(span)], axis=0),
        preferred_element_type=jnp.float32,
    ).astype(jnp.bfloat16)
    energies = jnp.concatenate([left_e_ref[first + t] for t in range(span)], axis=1)
    e_share[...] = jnp.sum(jnp.where(share_mask, energies, 0.0), axis=1, keepdims=True)
    for load in loads[3:]:
        load.wait()

    def apply_sector(n):
        sector = sector_of(n)
        size_now = tables[3, sector]
        first, offset = window_of(tables[2, sector])
        place = lax.broadcasted_iota(jnp.int32, (window, wide), 0)
        column = lax.broadcasted_iota(jnp.int32, (window, wide), 1)
        at_low = ((place == column + offset) & (column < size_now)).astype(jnp.bfloat16)
        moved = column - shift
        at_high = (
            (place == moved + offset) & (moved >= 0) & (moved < size_now)
        ).astype(jnp.bfloat16)
        block = jnp.concatenate([slab[first + t] for t in range(span)], axis=1)
        psi_pad[0] = jnp.dot(block, at_low, preferred_element_type=jnp.float32).astype(jnp.bfloat16)
        psi_pad[1] = jnp.dot(block, at_high, preferred_element_type=jnp.float32).astype(
            jnp.bfloat16
        )
        right_pad[0:widest, :] = rbuf[n]
        for q in range(sec_dev):
            at = q * widest
            even, odd = (
                jnp.dot(
                    left[:, parity, q].reshape(half_slots * widest, widest),
                    psi_pad[parity, at : at + widest, :],
                    preferred_element_type=jnp.float32,
                ).astype(jnp.bfloat16)
                for parity in range(2)
            )
            for p in range(half_slots):
                within = slice(p * widest, (p + 1) * widest)
                base = 2 * p * widest
                images[at : at + widest, base : base + LANE] = even[within, :LANE]
                images[at : at + widest, base + LANE : base + 2 * LANE] = (
                    even[within, LANE:] + odd[within, :LANE]
                )
                images[at : at + widest, base + 2 * LANE : base + 3 * LANE] = odd[within, LANE:]
        terms[...] = lax.dot_general(
            images[...], right_pad[...], (((1,), (1,)), ((), ())),
            preferred_element_type=jnp.float32,
        )
        for k in range(vectors):
            block = jnp.concatenate([vec[k, first + t] for t in range(span)], axis=1)
            spread[k] = jnp.dot(
                block, at_low, preferred_element_type=jnp.float32
            ).astype(jnp.bfloat16)
        step = 32

        def fold(idx, totals):
            at = pl.multiple_of(idx * step, step)
            values = terms[pl.ds(at, step), :]
            placed[sector, pl.ds(at, step), :] = values.astype(jnp.bfloat16)
            new = []
            for k in range(vectors):
                product = spread[k, pl.ds(at, step), :].astype(jnp.float32) * values
                folded = sum(
                    product[r : r + 8, c : c + LANE]
                    for r in range(0, step, 8) for c in range(0, wide, LANE)
                )
                new.append(totals[k] + folded)
            return tuple(new)

        totals = lax.fori_loop(
            0, rows // step, fold, tuple(acc[k] for k in range(vectors)), unroll=4
        )
        for k in range(vectors):
            acc[k] = totals[k]

    def y_copy(c):
        return remote(
            part.at[c, :, 1 - side], pair_in.at[c], y_s.at[c], y_r.at[c], {"ops": peer}
        )

    def outer_copy(c, k, target):
        return remote(
            sending.at[c, k], outer_in.at[c, k], outer_s.at[c, k], outer_r.at[c, k],
            {"ops": target},
        )

    def cols_of(c):
        return pl.ds(base_of(c), CHUNK)

    def gath_copy(c, k, source, target):
        block = out_ref.at[source, :, cols_of(c)]
        return remote(block, block, gath_s.at[c, k], gath_r.at[c, k], {"ops": target})

    def fwd_copy(c, k, source):
        block = out_ref.at[source, :, cols_of(c)]
        return remote(block, block, fwd_s.at[c, k], fwd_r.at[c, k], {"ops": peer})

    def place_chunk(c):
        base = base_of(c)
        low = jnp.int32(0)
        for r in range(sectors):
            low = low + (tables[2, r] + tables[3, r] <= base).astype(jnp.int32)
        low = jnp.minimum(low, sectors - overlap)
        source = lax.broadcasted_iota(jnp.int32, (wide, CHUNK), 0)
        target = lax.broadcasted_iota(jnp.int32, (wide, CHUNK), 1)
        for m in range(overlap):
            moved = source + (tables[2, low + m] - base)
            pick[m * wide : (m + 1) * wide, :] = (
                (moved == target) & (source < tables[3, low + m])
            ).astype(jnp.bfloat16)
        found = jnp.concatenate([placed[low + m] for m in range(overlap)], axis=1)
        value = jnp.dot(found, pick[...], preferred_element_type=jnp.float32)
        part[c] = value.reshape(outer, 2, share, CHUNK).astype(jnp.bfloat16)
        y_copy(c).start()

    def add_pair(c):
        y_copy(c).wait_recv()
        for k in range(outer - 1):
            dest = lax.rem(row + k + 1, outer)
            sending[c, k] = (
                part[c, dest, side].astype(jnp.float32) + pair_in[c, dest].astype(jnp.float32)
            ).astype(jnp.bfloat16)
            outer_copy(c, k, dest * 2 + side).start()

    def finish(c):
        for k in range(outer - 1):
            outer_copy(c, k, peer).wait_recv()
        cols = cols_of(c)
        total = part[c, row, side].astype(jnp.float32) + pair_in[c, row].astype(jnp.float32)
        for k in range(outer - 1):
            total = total + outer_in[c, k].astype(jnp.float32)
        diagonal = (e_share[...] + right_e_ref[0:1, cols]) * psi_share[:, cols].astype(jnp.float32)
        out_ref[me, :, cols] = (total + diagonal).astype(jnp.bfloat16)
        for k in range(outer - 1):
            gath_copy(c, k, me, lax.rem(row + k + 1, outer) * 2 + side).start()
        fwd_copy(c, outer - 1, me).start()
        for k in range(vectors):
            product = vec_share[k, :, cols].astype(jnp.float32) * diagonal
            acc[k] += sum(
                product[r : r + 8, at : at + LANE]
                for r in range(0, share, 8) for at in range(0, CHUNK, LANE)
            )

    def pass_on(c):
        for k in range(outer - 1):
            source = lax.rem(row - k - 1 + outer, outer) * 2 + side
            gath_copy(c, k, source, peer).wait_recv()
            fwd_copy(c, k, source).start()

    def done(n):
        return jnp.maximum(bond_dim - widest * (sectors - 1 - n), 0) // CHUNK

    def slot(n, carry):
        @pl.when(n >= half_sectors)
        def _():
            remote(
                rbuf.at[n, :, my_half], rbuf.at[n, :, my_half],
                x_s.at[0], x_r.at[n - half_sectors], {"site": across},
            ).wait_recv()
            forward(n, my_half).start()
            forward(n, peer_half).wait_recv()

        apply_sector(n)

        @pl.when(done(n) > done(n - 1))
        def _():
            place_chunk(done(n) - 1)

        @pl.when((done(n - 1) > done(n - 2)) & (n >= 1))
        def _():
            add_pair(done(n - 1) - 1)

        @pl.when((done(n - 2) > done(n - 3)) & (n >= 2))
        def _():
            finish(done(n - 2) - 1)

        @pl.when((done(n - 3) > done(n - 4)) & (n >= 3))
        def _():
            pass_on(done(n - 3) - 1)

        return carry

    lax.fori_loop(0, sectors, slot, 0)

    def plan(n):
        now = max(bond_dim - widest * (sectors - 1 - n), 0) // CHUNK
        before = max(bond_dim - widest * (sectors - n), 0) // CHUNK
        return now - 1 if now > before else None

    last = sectors - 1
    for stage, n in (
        (add_pair, last), (finish, last - 1), (pass_on, last - 2), (finish, last),
    ):
        c = plan(n)
        if c is not None:
            stage(c)

    corr_mine[...] = acc[...]
    corr_copies = []
    for k in range(1, groups):
        copy = remote(
            corr_mine, corr_ops.at[k], ops_s.at[k], ops_r.at[k], {"ops": lax.rem(me + k, groups)}
        )
        copy.start()
        corr_copies.append(copy)
    corr_ops[0] = corr_mine[...]

    for n in (last - 1, last):
        c = plan(n)
        if c is not None:
            pass_on(c)

    for copy in corr_copies:
        copy.wait_recv()

    def corr_add(g, total):
        return total + corr_ops[lax.rem(me - g + groups, groups)]

    corr_sites[0] = lax.fori_loop(0, groups, corr_add, jnp.zeros(acc.shape, jnp.float32))
    site_copies = []
    for k in range(1, sites):
        copy = remote(
            corr_sites.at[0], corr_sites.at[k], site_s.at[k], site_r.at[k],
            {"site": lax.rem(here + k, sites)},
        )
        copy.start()
        site_copies.append(copy)

    def last_waits(c, carry):
        fwd_copy(c, outer - 1, peer).wait_recv()
        for k in range(outer - 1):
            source = lax.rem(row - k - 1 + outer, outer) * 2 + 1 - side
            fwd_copy(c, k, source).wait_recv()
        y_copy(c).wait_send()
        for k in range(outer - 1):
            outer_copy(c, k, peer).wait_send()
            gath_copy(c, k, me, peer).wait_send()
            fwd_copy(c, k, me).wait_send()
        fwd_copy(c, outer - 1, me).wait_send()
        return carry

    lax.fori_loop(0, chunks, last_waits, 0)

    for copy in site_copies:
        copy.wait_recv()

    def site_add(g, total):
        return total + corr_sites[lax.rem(here - g + sites, sites)]

    corr = lax.fori_loop(0, sites, site_add, jnp.zeros(acc.shape, jnp.float32))
    for k in range(vectors):
        corr_out[k] = jnp.sum(corr[k])

    def x_waits(n, carry):
        to_across(n).wait_send()
        forward(n + half_sectors, my_half).wait_send()
        return carry

    lax.fori_loop(0, half_sectors, x_waits, 0)

    def pair_waits(w, carry):
        to_pair(order_of(w)).wait_send()
        return carry

    lax.fori_loop(0, sec_dev, pair_waits, 0)
    for copy in corr_copies + site_copies:
        copy.wait_send()


def local(
    wavefunction,
    left_blocks,
    right_blocks,
    left_sector,
    right_sector,
    term_count,
    left_energy,
    right_energy,
    subspace,
):
    slots, sec_dev, widest = left_blocks.shape[0], left_blocks.shape[1], left_blocks.shape[2]
    bond_dim = wavefunction.shape[0]
    vectors = subspace.shape[0]
    rows = sec_dev * widest
    sites = lax.axis_size("site")
    groups = lax.axis_size("ops")
    sectors = sec_dev * sites
    wide = round_up(widest, 256)
    window = round_up(widest + LANE - 1, LANE)
    share = rows // groups
    outer = groups // 2
    chunks = bond_dim // CHUNK
    tiles = bond_dim // LANE
    half_sectors = sectors // 2
    outside = -(-(bond_dim - CHUNK - 2 * (widest - 1)) // widest)
    overlap = min(sectors, sectors - outside)

    assert sites == 4 and slots % 4 == 0 and 2 * (wide - widest) == LANE and wide == 2 * LANE

    labels = jnp.arange(sectors, dtype=jnp.int32)
    ids = jnp.stack([left_sector, right_sector])
    starts = jnp.sum((ids[:, None, :] < labels[None, :, None]).astype(jnp.int32), axis=2)
    sizes = jnp.sum((ids[:, None, :] == labels[None, :, None]).astype(jnp.int32), axis=2)
    tables = jnp.stack([starts, sizes], axis=1).reshape(4, sectors)

    vmem = pl.BlockSpec(memory_space=pltpu.VMEM)
    smem = pl.BlockSpec(memory_space=pltpu.SMEM)
    hbm = pl.BlockSpec(memory_space=pl.ANY)
    dma = pltpu.SemaphoreType.DMA
    bf16, f32 = jnp.bfloat16, jnp.float32
    sigma, corr = pl.pallas_call(
        functools.partial(step_kernel, groups, sites),
        out_shape=(
            jax.ShapeDtypeStruct((groups, share, bond_dim), bf16),
            jax.ShapeDtypeStruct((vectors,), f32),
        ),
        in_specs=[smem, smem, hbm, hbm, hbm, hbm, hbm, vmem, vmem],
        out_specs=(vmem, smem),
        scratch_shapes=[
            pltpu.VMEM((slots // 2, 2, sec_dev, widest, widest), bf16),
            pltpu.VMEM((slots, sec_dev, widest, widest), bf16),
            pltpu.VMEM((tiles, LANE, bond_dim), bf16),
            pltpu.VMEM((vectors, tiles, rows, LANE), bf16),
            pltpu.VMEM((vectors, share, bond_dim), bf16),
            pltpu.VMEM((tiles, rows, LANE), bf16),
            pltpu.VMEM((share, bond_dim), bf16),
            pltpu.VMEM((share, 1), f32),
            pltpu.VMEM((sectors, widest, slots * widest), bf16),
            pltpu.VMEM((wide, slots * widest), bf16),
            pltpu.VMEM((2, rows, wide), bf16),
            pltpu.VMEM((rows, slots * widest), bf16),
            pltpu.VMEM((rows, wide), f32),
            pltpu.VMEM((vectors, rows, wide), bf16),
            pltpu.VMEM((sectors, rows, wide), bf16),
            pltpu.VMEM((overlap * wide, CHUNK), bf16),
            pltpu.VMEM((chunks, outer, 2, share, CHUNK), bf16),
            pltpu.VMEM((chunks, outer, share, CHUNK), bf16),
            pltpu.VMEM((chunks, outer - 1, share, CHUNK), bf16),
            pltpu.VMEM((chunks, outer - 1, share, CHUNK), bf16),
            pltpu.VMEM((vectors, 8, LANE), f32),
            pltpu.VMEM((vectors, 8, LANE), f32),
            pltpu.VMEM((groups, vectors, 8, LANE), f32),
            pltpu.VMEM((sites, vectors, 8, LANE), f32),
            dma((4 + vectors * tiles,)),
            dma((half_sectors,)), dma((half_sectors,)),
            dma((half_sectors,)), dma((half_sectors,)),
            dma((half_sectors,)), dma((half_sectors,)),
            dma((chunks,)), dma((chunks,)),
            dma((chunks, outer)), dma((chunks, outer)),
            dma((chunks, outer)), dma((chunks, outer)),
            dma((chunks, outer)), dma((chunks, outer)),
            dma((groups,)), dma((groups,)),
            dma((sites,)), dma((sites,)),
        ],
        compiler_params=pltpu.CompilerParams(
            collective_id=0, has_side_effects=True, vmem_limit_bytes=66_900_000
        ),
        name="davidson_step",
    )(
        tables,
        term_count,
        left_blocks.reshape(slots // 2, 2, sec_dev, widest, widest),
        right_blocks,
        wavefunction.reshape(tiles, LANE, bond_dim),
        subspace.reshape(vectors, rows, bond_dim),
        subspace.reshape(vectors, groups, share, bond_dim),
        left_energy.reshape(tiles, 1, LANE),
        right_energy[None, :],
    )
    return (sigma.reshape(sec_dev, widest, bond_dim), corr)


def solution(mesh):
    in_specs = (
        P(),
        P("ops", "site", None, None),
        P("ops", "site", None, None),
        P(),
        P(),
        P("ops"),
        P(),
        P(),
        P(None, "site", None, None),
    )
    out_specs = (P("site", None, None), P())
    return jax.shard_map(local, mesh=mesh, in_specs=in_specs, out_specs=out_specs, check_vma=False)
```

time: 249 us -> 142 us (0.57)
  Pallas kernels: 195 us -> 134 us
  other arithmetic: 24.4 us -> 0.91 us
  local copies, waits for them, and re-layouts: 19.8 us -> 5.07 us
  between operations: 9.08 us -> 1.3 us
    pallas_call x4 -> x1, Pallas kernels: 195 us -> 134 us  [local(): pl.pallas_call(functools.partial(step_kernel, groups, sites), out_shape=(...]
    reduce_sum x4 -> x1, other arithmetic: 8.88 us -> 0.18 us  [local(): jnp.sum((ids[:, None, :] < labels[None, :, None]).astype(jnp.int32), axis=2)]
    select_n x2 -> x0, other arithmetic: 6.66 us -> none  [the longest x1 3.53 us: local(): left = jnp.where(keep, left_blocks, jnp.zeros((), left_blocks.dtype))]
    reshape x2 -> x0, local copies, waits for them, and re-layouts: 5.76 us -> none  [the longest x1 3.76 us: local(): right_blocks.transpose(1, 2, 0, 3).reshape(sec_dev, widest, slots * widest)]
    lt x9 -> x0, other arithmetic: 5.03 us -> none  [the longest x8 5.02 us: local(): jnp.arange(widest, dtype=jnp.int32) < left_size[first_sector + within]]
    mul x1 -> x0, other arithmetic: 3.34 us -> none  [local(): (energy[:, None] + right_energy[None, :]) * psi_mine.astype(jnp.float32)]
    unnamed x11 -> x4, local copies, waits for them, and re-layouts: 6.59 us -> 4.49 us
where the time goes in v1:
time: 142 us; the launch traced here: 141 us
  Pallas kernels  134 us (94%)
  local copies, waits for them, and re-layouts  5.07 us (4%)
    pallas_call x1, Pallas kernels, local(): pl.pallas_call(functools.partial(step_kernel, groups, sites), out_shape=(...  134 us
    unnamed x4, local copies, waits for them, and re-layouts  4.49 us

profile of v1, /device:TPU:0, one launch (start us, length us, event | category | flops | bytes accessed | tf_op | source)
XLA Modules:
  0.0 141.5 jit_solution(10509350169833649523)
XLA Ops:
  1.3 0.7 pad_add_fusion
  2.0 0.2 convert_reduce_fusion.1
  2.2 0.6 copy.12
  2.8 134.2 %davidson_step.1 = (bf16[8,96,2048]{2,1,0:T(8,128)(2,1)}, f32[2]{0:T(128)}) custom-call(s32[4,16]{1,0:T(4,128)} %bitcast.19, s32[1]{0:T(128)S(6)} %copy.15.count, bf16[4,2,4,192,192]{4,3,2,1,0:T(8,128)(2,1)} %bitcast.16, bf16[8,4,192,192]{3,2,1,0:T(8,128)(2,1)} %right_hbm.1, bf16[16,128,2048]{2,1,0:T(8,128)(2,1)} %bitcast.14, ...), custom_call_target="tpu_custom_call" | custom-call | tf_op jit(solution)/shard_map/davidson_step/pallas_call | solution.py:525
  137.0 0.0 copy-start
  137.0 4.0 %copy.16 = bf16[4,192,2048]{2,1,0:T(8,128)(2,1)} copy(bf16[4,192,2048]{2,1,0:T(8,128)(2,1)} %bitcast.15) | data formatting | bytes 6291456
  141.0 0.0 copy-done
  141.0 0.5 copy.17
  (1 shorter events, 0.0 us)
Async XLA Ops:
  137.0 4.0 %copy-start = (f32[2]{0:T(128)S(1)}, f32[2]{0:T(128)}, u32[]{:S(2)}) copy-start(f32[2]{0:T(128)} %get-tuple-element.11) | copy-start | bytes 28

commit v2 on v1

--- a/solution.py
+++ b/solution.py
@@ -28,17 +28,16 @@
 ):
     half_slots, _, sec_dev, widest, _ = left.shape
     slots = 2 * half_slots
-    rows = slab.shape[1]
+    vectors, halves, tiles, rows, _ = vec.shape
     bond_dim = psi.shape[2]
-    vectors = vec.shape[0]
+    sec_half = sec_dev // halves
     sectors = sec_dev * sites
     wide = psi_pad.shape[2]
     shift = wide - widest
     window = round_up(widest + LANE - 1, LANE)
     outer = groups // 2
     share = rows // groups
-    chunks = bond_dim // CHUNK
-    tiles = bond_dim // LANE
+    items = bond_dim // CHUNK * halves
     half_sectors = sectors // 2
     half_cols = slots * widest // 2
     outside = -(-(bond_dim - CHUNK - 2 * (widest - 1)) // widest)
@@ -73,16 +72,17 @@
         pltpu.make_async_copy(right_hbm, right, load_s.at[0]),
         pltpu.make_async_copy(left_hbm, left, load_s.at[1]),
         pltpu.make_async_copy(psi_hbm, psi, load_s.at[2]),
-        pltpu.make_async_copy(share_hbm.at[:, me], vec_share, load_s.at[3]),
+        pltpu.make_async_copy(share_hbm.at[:, :, me], vec_share, load_s.at[3]),
     ]
     for k in range(vectors):
-        for t in range(tiles):
-            loads.append(
-                pltpu.make_async_copy(
-                    vec_hbm.at[k, :, t * LANE : (t + 1) * LANE], vec.at[k, t],
-                    load_s.at[4 + k * tiles + t],
+        for h in range(halves):
+            for t in range(tiles):
+                loads.append(
+                    pltpu.make_async_copy(
+                        vec_hbm.at[k, h, :, t * LANE : (t + 1) * LANE], vec.at[k, h, t],
+                        load_s.at[4 + (k * halves + h) * tiles + t],
+                    )
                 )
-            )
     for load in loads:
         load.start()
 
@@ -101,6 +101,9 @@
     lower = (lane_in == lane_out).astype(jnp.bfloat16)
     upper = (lane_in + shift == lane_out).astype(jnp.bfloat16)
 
+    right_pad[widest:, :] = jnp.zeros((wide - widest, slots * widest), jnp.bfloat16)
+    placed[...] = jnp.zeros_like(placed)
+    acc[...] = jnp.zeros_like(acc)
     loads[0].wait()
 
     def pack(w, carry):
@@ -148,19 +151,6 @@
 
     lax.fori_loop(0, sec_dev, start_pair, 0)
 
-    def start_across(idx, carry):
-        n = half_sectors - 1 - idx
-        owner = sector_of(n) // sec_dev
-
-        @pl.when(owner != here)
-        def _():
-            to_pair(n).wait_recv()
-
-        to_across(n).start()
-        return carry
-
-    lax.fori_loop(0, half_sectors, start_across, 0)
-
     first_sector = here * sec_dev
 
     span = window // LANE
@@ -168,10 +158,6 @@
     def window_of(start):
         first = jnp.minimum(start // LANE, tiles - span)
         return first, start - first * LANE
-
-    right_pad[...] = jnp.zeros_like(right_pad)
-    placed[...] = jnp.zeros_like(placed)
-    acc[...] = jnp.zeros_like(acc)
 
     loads[1].wait()
     live_count = count[0]
@@ -201,27 +187,43 @@
             choose, jnp.concatenate([psi[first + t] for t in range(span)], axis=0),
             preferred_element_type=jnp.float32,
         ).astype(jnp.bfloat16)
+        h, at = q // sec_half, q % sec_half * widest
         for t in range(tiles):
-            slab[t, q * widest : (q + 1) * widest, :] = found[:, t * LANE : (t + 1) * LANE]
-
-    share_at = me * share
-    share_q = first_sector + share_at // widest
-    share_off = share_at % widest
-    first, offset = window_of(tables[0, share_q])
-    out_row = lax.broadcasted_iota(jnp.int32, (share, window), 0) + share_off
-    in_row = lax.broadcasted_iota(jnp.int32, (share, window), 1)
-    share_mask = (in_row == out_row + offset) & (out_row < tables[1, share_q])
-    choose = share_mask.astype(jnp.bfloat16)
-    psi_share[...] = jnp.dot(
-        choose, jnp.concatenate([psi[first + t] for t in range(span)], axis=0),
-        preferred_element_type=jnp.float32,
-    ).astype(jnp.bfloat16)
-    energies = jnp.concatenate([left_e_ref[first + t] for t in range(span)], axis=1)
-    e_share[...] = jnp.sum(jnp.where(share_mask, energies, 0.0), axis=1, keepdims=True)
+            slab[h, t, at : at + widest, :] = found[:, t * LANE : (t + 1) * LANE]
+
+    for h in range(halves):
+        share_at = h * rows + me * share
+        share_q = first_sector + share_at // widest
+        share_off = share_at % widest
+        first, offset = window_of(tables[0, share_q])
+        out_row = lax.broadcasted_iota(jnp.int32, (share, window), 0) + share_off
+        in_row = lax.broadcasted_iota(jnp.int32, (share, window), 1)
+        share_mask = (in_row == out_row + offset) & (out_row < tables[1, share_q])
+        choose = share_mask.astype(jnp.bfloat16)
+        psi_share[h] = jnp.dot(
+            choose, jnp.concatenate([psi[first + t] for t in range(span)], axis=0),
+            preferred_element_type=jnp.float32,
+        ).astype(jnp.bfloat16)
+        energies = jnp.concatenate([left_e_ref[first + t] for t in range(span)], axis=1)
+        e_share[h] = jnp.sum(jnp.where(share_mask, energies, 0.0), axis=1, keepdims=True)
     for load in loads[3:]:
         load.wait()
 
-    def apply_sector(n):
+    def start_across(idx, carry):
+        n = half_sectors - 1 - idx
+        owner = sector_of(n) // sec_dev
+
+        @pl.when(owner != here)
+        def _():
+            to_pair(n).wait_recv()
+
+        to_across(n).start()
+        return carry
+
+    lax.fori_loop(0, half_sectors, start_across, 0)
+
+
+    def apply_sector(n, h):
         sector = sector_of(n)
         size_now = tables[3, sector]
         first, offset = window_of(tables[2, sector])
@@ -232,17 +234,17 @@
         at_high = (
             (place == moved + offset) & (moved >= 0) & (moved < size_now)
         ).astype(jnp.bfloat16)
-        block = jnp.concatenate([slab[first + t] for t in range(span)], axis=1)
+        block = jnp.concatenate([slab[h, first + t] for t in range(span)], axis=1)
         psi_pad[0] = jnp.dot(block, at_low, preferred_element_type=jnp.float32).astype(jnp.bfloat16)
         psi_pad[1] = jnp.dot(block, at_high, preferred_element_type=jnp.float32).astype(
             jnp.bfloat16
         )
         right_pad[0:widest, :] = rbuf[n]
-        for q in range(sec_dev):
+        for q in range(sec_half):
             at = q * widest
             even, odd = (
                 jnp.dot(
-                    left[:, parity, q].reshape(half_slots * widest, widest),
+                    left[:, parity, h * sec_half + q].reshape(half_slots * widest, widest),
                     psi_pad[parity, at : at + widest, :],
                     preferred_element_type=jnp.float32,
                 ).astype(jnp.bfloat16)
@@ -261,7 +263,7 @@
             preferred_element_type=jnp.float32,
         )
         for k in range(vectors):
-            block = jnp.concatenate([vec[k, first + t] for t in range(span)], axis=1)
+            block = jnp.concatenate([vec[k, h, first + t] for t in range(span)], axis=1)
             spread[k] = jnp.dot(
                 block, at_low, preferred_element_type=jnp.float32
             ).astype(jnp.bfloat16)
@@ -270,7 +272,7 @@
         def fold(idx, totals):
             at = pl.multiple_of(idx * step, step)
             values = terms[pl.ds(at, step), :]
-            placed[sector, pl.ds(at, step), :] = values.astype(jnp.bfloat16)
+            placed[h, sector, pl.ds(at, step), :] = values.astype(jnp.bfloat16)
             new = []
             for k in range(vectors):
                 product = spread[k, pl.ds(at, step), :].astype(jnp.float32) * values
@@ -287,30 +289,30 @@
         for k in range(vectors):
             acc[k] = totals[k]
 
-    def y_copy(c):
+    def y_copy(e):
         return remote(
-            part.at[c, :, 1 - side], pair_in.at[c], y_s.at[c], y_r.at[c], {"ops": peer}
-        )
-
-    def outer_copy(c, k, target):
+            part.at[e, :, 1 - side], pair_in.at[e], y_s.at[e], y_r.at[e], {"ops": peer}
+        )
+
+    def outer_copy(e, k, target):
         return remote(
-            sending.at[c, k], outer_in.at[c, k], outer_s.at[c, k], outer_r.at[c, k],
+            sending.at[e, k], outer_in.at[e, k], outer_s.at[e, k], outer_r.at[e, k],
             {"ops": target},
         )
 
-    def cols_of(c):
-        return pl.ds(base_of(c), CHUNK)
-
-    def gath_copy(c, k, source, target):
-        block = out_ref.at[source, :, cols_of(c)]
-        return remote(block, block, gath_s.at[c, k], gath_r.at[c, k], {"ops": target})
-
-    def fwd_copy(c, k, source):
-        block = out_ref.at[source, :, cols_of(c)]
-        return remote(block, block, fwd_s.at[c, k], fwd_r.at[c, k], {"ops": peer})
-
-    def place_chunk(c):
-        base = base_of(c)
+    def cols_of(e):
+        return pl.ds(base_of(e // halves), CHUNK)
+
+    def gath_copy(e, k, source, target):
+        block = out_ref.at[e % halves, source, :, cols_of(e)]
+        return remote(block, block, gath_s.at[e, k], gath_r.at[e, k], {"ops": target})
+
+    def fwd_copy(e, k, source):
+        block = out_ref.at[e % halves, source, :, cols_of(e)]
+        return remote(block, block, fwd_s.at[e, k], fwd_r.at[e, k], {"ops": peer})
+
+    def place_chunk(e):
+        base = base_of(e // halves)
         low = jnp.int32(0)
         for r in range(sectors):
             low = low + (tables[2, r] + tables[3, r] <= base).astype(jnp.int32)
@@ -322,50 +324,76 @@
             pick[m * wide : (m + 1) * wide, :] = (
                 (moved == target) & (source < tables[3, low + m])
             ).astype(jnp.bfloat16)
-        found = jnp.concatenate([placed[low + m] for m in range(overlap)], axis=1)
+        found = jnp.concatenate([placed[e % halves, low + m] for m in range(overlap)], axis=1)
         value = jnp.dot(found, pick[...], preferred_element_type=jnp.float32)
-        part[c] = value.reshape(outer, 2, share, CHUNK).astype(jnp.bfloat16)
-        y_copy(c).start()
-
-    def add_pair(c):
-        y_copy(c).wait_recv()
+        part[e] = value.reshape(outer, 2, share, CHUNK).astype(jnp.bfloat16)
+        y_copy(e).start()
+
+    def add_pair(e):
+        y_copy(e).wait_recv()
         for k in range(outer - 1):
             dest = lax.rem(row + k + 1, outer)
-            sending[c, k] = (
-                part[c, dest, side].astype(jnp.float32) + pair_in[c, dest].astype(jnp.float32)
+            sending[e, k] = (
+                part[e, dest, side].astype(jnp.float32) + pair_in[e, dest].astype(jnp.float32)
             ).astype(jnp.bfloat16)
-            outer_copy(c, k, dest * 2 + side).start()
-
-    def finish(c):
-        for k in range(outer - 1):
-            outer_copy(c, k, peer).wait_recv()
-        cols = cols_of(c)
-        total = part[c, row, side].astype(jnp.float32) + pair_in[c, row].astype(jnp.float32)
-        for k in range(outer - 1):
-            total = total + outer_in[c, k].astype(jnp.float32)
-        diagonal = (e_share[...] + right_e_ref[0:1, cols]) * psi_share[:, cols].astype(jnp.float32)
-        out_ref[me, :, cols] = (total + diagonal).astype(jnp.bfloat16)
-        for k in range(outer - 1):
-            gath_copy(c, k, me, lax.rem(row + k + 1, outer) * 2 + side).start()
-        fwd_copy(c, outer - 1, me).start()
+            outer_copy(e, k, dest * 2 + side).start()
+
+    def diagonal_of(e):
+        cols = cols_of(e)
+        h = e % halves
+        return (e_share[h] + right_e_ref[0:1, cols]) * psi_share[h, :, cols].astype(jnp.float32)
+
+    def project_diagonal(e):
+        diagonal = diagonal_of(e)
         for k in range(vectors):
-            product = vec_share[k, :, cols].astype(jnp.float32) * diagonal
+            product = vec_share[k, e % halves, :, cols_of(e)].astype(jnp.float32) * diagonal
             acc[k] += sum(
                 product[r : r + 8, at : at + LANE]
                 for r in range(0, share, 8) for at in range(0, CHUNK, LANE)
             )
 
-    def pass_on(c):
+    def finish(e):
+        for k in range(outer - 1):
+            outer_copy(e, k, peer).wait_recv()
+        total = part[e, row, side].astype(jnp.float32) + pair_in[e, row].astype(jnp.float32)
+        for k in range(outer - 1):
+            total = total + outer_in[e, k].astype(jnp.float32)
+        out_ref[e % halves, me, :, cols_of(e)] = (total + diagonal_of(e)).astype(jnp.bfloat16)
+        for k in range(outer - 1):
+            gath_copy(e, k, me, lax.rem(row + k + 1, outer) * 2 + side).start()
+        fwd_copy(e, outer - 1, me).start()
+
+    def pass_on(e):
         for k in range(outer - 1):
             source = lax.rem(row - k - 1 + outer, outer) * 2 + side
-            gath_copy(c, k, source, peer).wait_recv()
-            fwd_copy(c, k, source).start()
+            gath_copy(e, k, source, peer).wait_recv()
+            fwd_copy(e, k, source).start()
+
+    local_slots = half_sectors * halves
+    slots_all = sectors * halves
+
+    def slot_of(m):
+        late = jnp.maximum(m - local_slots, 0)
+        early = m < local_slots
+        n = jnp.where(early, m % half_sectors, half_sectors + late // halves)
+        return n, jnp.where(early, m // half_sectors, late % halves)
 
     def done(n):
         return jnp.maximum(bond_dim - widest * (sectors - 1 - n), 0) // CHUNK
 
-    def slot(n, carry):
-        @pl.when(n >= half_sectors)
+    def run_stage(stage, m):
+        n, h = slot_of(jnp.maximum(m, 0))
+
+        @pl.when((m >= 0) & (m < slots_all) & (done(n) > done(n - 1)))
+        def _():
+            stage((done(n) - 1) * halves + h)
+
+    stages = ((place_chunk, 0), (add_pair, 1), (finish, 3), (pass_on, 5))
+
+    def slot(m, carry):
+        n, h = slot_of(m)
+
+        @pl.when((m >= local_slots) & (h == 0))
         def _():
             remote(
                 rbuf.at[n, :, my_half], rbuf.at[n, :, my_half],
@@ -374,40 +402,18 @@
             forward(n, my_half).start()
             forward(n, peer_half).wait_recv()
 
-        apply_sector(n)
-
-        @pl.when(done(n) > done(n - 1))
+        apply_sector(n, h)
+
+        @pl.when((m >= local_slots) & (m < local_slots + items))
         def _():
-            place_chunk(done(n) - 1)
-
-        @pl.when((done(n - 1) > done(n - 2)) & (n >= 1))
-        def _():
-            add_pair(done(n - 1) - 1)
-
-        @pl.when((done(n - 2) > done(n - 3)) & (n >= 2))
-        def _():
-            finish(done(n - 2) - 1)
-
-        @pl.when((done(n - 3) > done(n - 4)) & (n >= 3))
-        def _():
-            pass_on(done(n - 3) - 1)
-
-        return carry
-
-    lax.fori_loop(0, sectors, slot, 0)
-
-    def plan(n):
-        now = max(bond_dim - widest * (sectors - 1 - n), 0) // CHUNK
-        before = max(bond_dim - widest * (sectors - n), 0) // CHUNK
-        return now - 1 if now > before else None
-
-    last = sectors - 1
-    for stage, n in (
-        (add_pair, last), (finish, last - 1), (pass_on, last - 2), (finish, last),
-    ):
-        c = plan(n)
-        if c is not None:
-            stage(c)
+            project_diagonal(m - local_slots)
+
+        for stage, lag in stages:
+            run_stage(stage, m - lag)
+
+        return carry
+
+    lax.fori_loop(0, slots_all, slot, 0)
 
     corr_mine[...] = acc[...]
     corr_copies = []
@@ -419,10 +425,12 @@
         corr_copies.append(copy)
     corr_ops[0] = corr_mine[...]
 
-    for n in (last - 1, last):
-        c = plan(n)
-        if c is not None:
-            pass_on(c)
+    def drain(m, carry):
+        for stage, lag in stages[1:]:
+            run_stage(stage, m - lag)
+        return carry
+
+    lax.fori_loop(slots_all, slots_all + 1, drain, 0)
 
     for copy in corr_copies:
         copy.wait_recv()
@@ -439,6 +447,8 @@
         )
         copy.start()
         site_copies.append(copy)
+
+    lax.fori_loop(slots_all + 1, slots_all + 5, drain, 0)
 
     def last_waits(c, carry):
         fwd_copy(c, outer - 1, peer).wait_recv()
@@ -453,7 +463,7 @@
         fwd_copy(c, outer - 1, me).wait_send()
         return carry
 
-    lax.fori_loop(0, chunks, last_waits, 0)
+    lax.fori_loop(0, items, last_waits, 0)
 
     for copy in site_copies:
         copy.wait_recv()
@@ -501,9 +511,11 @@
     sectors = sec_dev * sites
     wide = round_up(widest, 256)
     window = round_up(widest + LANE - 1, LANE)
+    outer = groups // 2
+    halves = 2 if groups > 99 and rows // 2 % (16 * groups) == 0 and sec_dev % 2 == 0 else 1
+    rows = rows // halves
     share = rows // groups
-    outer = groups // 2
-    chunks = bond_dim // CHUNK
+    items = bond_dim // CHUNK * halves
     tiles = bond_dim // LANE
     half_sectors = sectors // 2
     outside = -(-(bond_dim - CHUNK - 2 * (widest - 1)) // widest)
@@ -525,7 +537,7 @@
     sigma, corr = pl.pallas_call(
         functools.partial(step_kernel, groups, sites),
         out_shape=(
-            jax.ShapeDtypeStruct((groups, share, bond_dim), bf16),
+            jax.ShapeDtypeStruct((halves, groups, share, bond_dim), bf16),
             jax.ShapeDtypeStruct((vectors,), f32),
         ),
         in_specs=[smem, smem, hbm, hbm, hbm, hbm, hbm, vmem, vmem],
@@ -534,35 +546,35 @@
             pltpu.VMEM((slots // 2, 2, sec_dev, widest, widest), bf16),
             pltpu.VMEM((slots, sec_dev, widest, widest), bf16),
             pltpu.VMEM((tiles, LANE, bond_dim), bf16),
-            pltpu.VMEM((vectors, tiles, rows, LANE), bf16),
-            pltpu.VMEM((vectors, share, bond_dim), bf16),
-            pltpu.VMEM((tiles, rows, LANE), bf16),
-            pltpu.VMEM((share, bond_dim), bf16),
-            pltpu.VMEM((share, 1), f32),
+            pltpu.VMEM((vectors, halves, tiles, rows, LANE), bf16),
+            pltpu.VMEM((vectors, halves, share, bond_dim), bf16),
+            pltpu.VMEM((halves, tiles, rows, LANE), bf16),
+            pltpu.VMEM((halves, share, bond_dim), bf16),
+            pltpu.VMEM((halves, share, 1), f32),
             pltpu.VMEM((sectors, widest, slots * widest), bf16),
             pltpu.VMEM((wide, slots * widest), bf16),
             pltpu.VMEM((2, rows, wide), bf16),
             pltpu.VMEM((rows, slots * widest), bf16),
             pltpu.VMEM((rows, wide), f32),
             pltpu.VMEM((vectors, rows, wide), bf16),
-            pltpu.VMEM((sectors, rows, wide), bf16),
+            pltpu.VMEM((halves, sectors, rows, wide), bf16),
             pltpu.VMEM((overlap * wide, CHUNK), bf16),
-            pltpu.VMEM((chunks, outer, 2, share, CHUNK), bf16),
-            pltpu.VMEM((chunks, outer, share, CHUNK), bf16),
-            pltpu.VMEM((chunks, outer - 1, share, CHUNK), bf16),
-            pltpu.VMEM((chunks, outer - 1, share, CHUNK), bf16),
+            pltpu.VMEM((items, outer, 2, share, CHUNK), bf16),
+            pltpu.VMEM((items, outer, share, CHUNK), bf16),
+            pltpu.VMEM((items, outer - 1, share, CHUNK), bf16),
+            pltpu.VMEM((items, outer - 1, share, CHUNK), bf16),
             pltpu.VMEM((vectors, 8, LANE), f32),
             pltpu.VMEM((vectors, 8, LANE), f32),
             pltpu.VMEM((groups, vectors, 8, LANE), f32),
             pltpu.VMEM((sites, vectors, 8, LANE), f32),
-            dma((4 + vectors * tiles,)),
+            dma((4 + vectors * halves * tiles,)),
             dma((half_sectors,)), dma((half_sectors,)),
             dma((half_sectors,)), dma((half_sectors,)),
             dma((half_sectors,)), dma((half_sectors,)),
-            dma((chunks,)), dma((chunks,)),
-            dma((chunks, outer)), dma((chunks, outer)),
-            dma((chunks, outer)), dma((chunks, outer)),
-            dma((chunks, outer)), dma((chunks, outer)),
+            dma((items,)), dma((items,)),
+            dma((items, outer)), dma((items, outer)),
+            dma((items, outer)), dma((items, outer)),
+            dma((items, outer)), dma((items, outer)),
             dma((groups,)), dma((groups,)),
             dma((sites,)), dma((sites,)),
         ],
@@ -576,8 +588,8 @@
         left_blocks.reshape(slots // 2, 2, sec_dev, widest, widest),
         right_blocks,
         wavefunction.reshape(tiles, LANE, bond_dim),
-        subspace.reshape(vectors, rows, bond_dim),
-        subspace.reshape(vectors, groups, share, bond_dim),
+        subspace.reshape(vectors, halves, rows, bond_dim),
+        subspace.reshape(vectors, halves, groups, share, bond_dim),
         left_energy.reshape(tiles, 1, LANE),
         right_energy[None, :],
     )

time: 142 us -> 130 us (0.915)
  Pallas kernels: 134 us -> 122 us
    pallas_call x1, Pallas kernels: 134 us -> 122 us  [local(): pl.pallas_call(functools.partial(step_kernel, groups, sites), out_shape=(...]
where the time goes in v2:
time: 130 us
  Pallas kernels  122 us (94%)
  local copies, waits for them, and re-layouts  5.07 us (4%)
  between operations  1.3 us (1%)
    pallas_call x1, Pallas kernels, local(): pl.pallas_call(functools.partial(step_kernel, groups, sites), out_shape=(...  122 us
    unnamed x4, local copies, waits for them, and re-layouts  4.49 us

profile of v2, /device:TPU:0, one launch (start us, length us, event | category | flops | bytes accessed | tf_op | source)
XLA Modules:
  0.0 129.7 jit_solution(11427338892967099926)
XLA Ops:
  1.3 0.7 pad_add_fusion
  2.0 0.2 convert_reduce_fusion.1
  2.2 0.6 copy.12
  2.8 122.4 %davidson_step.1 = (bf16[1,8,96,2048]{3,2,1,0:T(8,128)(2,1)}, f32[2]{0:T(128)}) custom-call(s32[4,16]{1,0:T(4,128)} %bitcast.19, s32[1]{0:T(128)S(6)} %copy.15.count, bf16[4,2,4,192,192]{4,3,2,1,0:T(8,128)(2,1)} %bitcast.16, bf16[8,4,192,192]{3,2,1,0:T(8,128)(2,1)} %right_hbm.1, bf16[16,128,2048]{2,1,0:T(8,128)(2,1)} %bitcast.14, ...), custom_call_target="tpu_custom_call" | custom-call | tf_op jit(solution)/shard_map/davidson_step/pallas_call | solution.py:537
  125.2 0.0 copy-start
  125.2 4.0 %copy.16 = bf16[4,192,2048]{2,1,0:T(8,128)(2,1)} copy(bf16[4,192,2048]{2,1,0:T(8,128)(2,1)} %bitcast.15) | data formatting | bytes 6291456
  129.2 0.0 copy-done
  129.2 0.5 copy.17
  (1 shorter events, 0.0 us)
Async XLA Ops:
  125.2 4.0 %copy-start = (f32[2]{0:T(128)S(1)}, f32[2]{0:T(128)}, u32[]{:S(2)}) copy-start(f32[2]{0:T(128)} %get-tuple-element.11) | copy-start | bytes 28

commit v3 on v2

--- a/solution.py
+++ b/solution.py
@@ -388,7 +388,7 @@
         def _():
             stage((done(n) - 1) * halves + h)
 
-    stages = ((place_chunk, 0), (add_pair, 1), (finish, 3), (pass_on, 5))
+    stages = ((place_chunk, 0), (add_pair, 1), (finish, 3), (pass_on, 6))
 
     def slot(m, carry):
         n, h = slot_of(m)
@@ -448,7 +448,7 @@
         copy.start()
         site_copies.append(copy)
 
-    lax.fori_loop(slots_all + 1, slots_all + 5, drain, 0)
+    lax.fori_loop(slots_all + 1, slots_all + 6, drain, 0)
 
     def last_waits(c, carry):
         fwd_copy(c, outer - 1, peer).wait_recv()

time: 130 us -> 130 us (level)
  no operation moved by 1% of the time
where the time goes in v3:
time: 130 us
  Pallas kernels  122 us (94%)
  local copies, waits for them, and re-layouts  5.07 us (4%)
  between operations  1.3 us (1%)
    pallas_call x1, Pallas kernels, local(): pl.pallas_call(functools.partial(step_kernel, groups, sites), out_shape=(...  122 us
    unnamed x4, local copies, waits for them, and re-layouts  4.49 us

profile of v3, /device:TPU:0, one launch (start us, length us, event | category | flops | bytes accessed | tf_op | source)
XLA Modules:
  0.0 129.7 jit_solution(6228174498533544814)
XLA Ops:
  1.3 0.7 pad_add_fusion
  2.0 0.2 convert_reduce_fusion.1
  2.2 0.6 copy.12
  2.8 122.4 %davidson_step.1 = (bf16[1,8,96,2048]{3,2,1,0:T(8,128)(2,1)}, f32[2]{0:T(128)}) custom-call(s32[4,16]{1,0:T(4,128)} %bitcast.19, s32[1]{0:T(128)S(6)} %copy.15.count, bf16[4,2,4,192,192]{4,3,2,1,0:T(8,128)(2,1)} %bitcast.16, bf16[8,4,192,192]{3,2,1,0:T(8,128)(2,1)} %right_hbm.1, bf16[16,128,2048]{2,1,0:T(8,128)(2,1)} %bitcast.14, ...), custom_call_target="tpu_custom_call" | custom-call | tf_op jit(solution)/shard_map/davidson_step/pallas_call | solution.py:537
  125.2 0.0 copy-start
  125.2 4.0 %copy.16 = bf16[4,192,2048]{2,1,0:T(8,128)(2,1)} copy(bf16[4,192,2048]{2,1,0:T(8,128)(2,1)} %bitcast.15) | data formatting | bytes 6291456
  129.2 0.0 copy-done
  129.2 0.5 copy.17
  (1 shorter events, 0.0 us)
Async XLA Ops:
  125.2 4.0 %copy-start = (f32[2]{0:T(128)S(1)}, f32[2]{0:T(128)}, u32[]{:S(2)}) copy-start(f32[2]{0:T(128)} %get-tuple-element.11) | copy-start | bytes 28
